TPU v7x, 256 devices: a whole 4x4x8 slice. The times are simulated.
256 devices in a mesh: dp: 128 (over z, y, x), mp: 2 (over core).
Axes of the slice: x: 4, y: 4, z: 8, core: 2. Of those that a mesh axis runs over, the one named last changes fastest.
Arguments:
- points: bfloat16 [131072, 1024], P(('dp', 'mp')), may hold values from -6 to 6
- centroids: bfloat16 [4096, 1024], P('mp'), may hold values from -6 to 6
- assign: int32 [131072], P(('dp', 'mp')), may hold values from 0 to 4095
- keep_mask: int32 [131072], P(('dp', 'mp')), may hold values 0 or 1
Outputs:
- new_centroids: float32 [4096, 1024], P('mp')
- row_cost: float32 [131072], P(('dp', 'mp'))
All inputs are finite; a program needn't handle non-finite values. No bound on the sum of `keep_mask` on one device may be relied on, other than what follows from the above.
Results may differ from a plain program's by a relative error of at most 0.0008.
Values may be sent and summed in bfloat16 or wider, within the bound.
No kernel may reach another device: no remote copies, remote signals or barrier semaphores. Data moves between devices by JAX's collectives and lax.ppermute only.
A program may use at most 128 MiB of HBM per device.

v0:
```python
import math

import jax
import jax.numpy as jnp
from jax import lax
from jax.sharding import PartitionSpec as P


def in_one_piece(arrays, axis, dim, along):
    widths = [math.prod(a.shape[along:]) for a in arrays]
    both = jnp.concatenate(
        [a.reshape(*a.shape[:along], w) for a, w in zip(arrays, widths)], axis=along
    )
    filled = lax.psum_scatter(both, axis, scatter_dimension=dim, tiled=True)
    parts = jnp.split(filled, [sum(widths[:k]) for k in range(1, len(widths))], axis=along)
    return tuple(
        (b.reshape(*filled.shape[:along], *a.shape[along:]) for a, b in zip(arrays, parts))
    )


def together(arrays, axis):
    ends = [0]
    for a in arrays:
        ends.append(ends[-1] + a.size)
    total = lax.psum(jnp.concatenate([a.ravel() for a in arrays]), axis)
    return tuple((total[b:e].reshape(a.shape) for a, b, e in zip(arrays, ends, ends[1:])))


def update(sums, counts, prior):
    fresh = sums / jnp.maximum(counts, 1.0)[:, None]
    return jnp.where(counts[:, None] > 0.5, fresh, prior)


def shards(points, centroids, assign, keep_mask):
    width = points.shape[1]
    point_f = points.astype(jnp.float32)
    point_sq = jnp.sum(point_f * point_f, axis=1)
    piece = lax.all_gather(centroids, "mp", axis=0, tiled=True)
    inner = lax.dot_general(
        points, piece, (((1,), (1,)), ((), ())), preferred_element_type=jnp.float32
    )
    piece_f = piece.astype(jnp.float32)
    cent_sq = jnp.sum(piece_f * piece_f, axis=1)
    dist = point_sq[:, None] - 2.0 * inner + cent_sq[None, :]
    row_cost = jnp.min(dist, axis=1) / width
    shard_rows = centroids.shape[0]
    mp_count = lax.axis_size("mp")
    total = shard_rows * mp_count
    weights = keep_mask.astype(jnp.float32)
    onehot = (jnp.arange(total, dtype=jnp.int32)[:, None] == assign[None, :]).astype(
        jnp.float32
    ) * weights[None, :]
    counts = jnp.sum(onehot, axis=1)
    sums = jnp.dot(onehot.astype(jnp.bfloat16), points, preferred_element_type=jnp.float32)
    part_sums, part_counts = tuple(
        (
            part.astype(jnp.float32)
            for part in in_one_piece(
                (sums.astype(jnp.bfloat16), counts.astype(jnp.bfloat16)), "mp", 0, 1
            )
        )
    )
    part_sums, part_counts = together((part_sums, part_counts), "dp")
    new_centroids = update(part_sums, part_counts, centroids.astype(jnp.float32))
    return (new_centroids, row_cost)


def solution(mesh):
    in_specs = (P(("dp", "mp"), None), P("mp", None), P(("dp", "mp")), P(("dp", "mp")))
    out_specs = (P("mp", None), P(("dp", "mp")))
    return jax.shard_map(shards, mesh=mesh, in_specs=in_specs, out_specs=out_specs, check_vma=False)
```

profile of v0, /device:TPU:1, one launch (start us, length us, event | category | flops | bytes accessed | tf_op | source)
XLA Modules:
  0.0 378.8 jit_solution(1815429311164236135)
XLA Ops:
  7.2 0.0 reduce-scatter.2.cloned.1.call-start
  7.2 0.7 convert_element_type.37
  7.9 1.7 select_reduce_fusion
  9.6 8.1 %convolution_convert_fusion = bf16[4096,1024]{0,1:T(8,128)(2,1)} fusion(bf16[512,1024]{1,0:T(8,128)(2,1)} %param.4, f32[512]{0:T(512)S(1)} %convert_element_type.37, s32[512]{0:T(512)} %param.6), kind=kOutput, calls=%fused_computation.7 | convolution fusion | flops 4303355904 | bytes 9441280 | tf_op jit(solution)/shard_map/dot_general | solution.py:54
  17.6 7.7 %pad_maximum_fusion = bf16[4096,1025]{0,1:T(8,128)(2,1)} fusion(bf16[4096,1]{0,1:T(2,128)(2,1)S(1)} %convert_element_type.41, bf16[4096,1024]{0,1:T(8,128)(2,1)} %convolution_convert_fusion), kind=kLoop, calls=%fused_computation.3 | loop fusion | flops 16793600 | bytes 16793600 | tf_op jit(solution)/shard_map/concatenate | solution.py:11
  25.4 0.0 reduce-scatter.2.cloned.1.call-update
  25.4 0.0 all-gather.2.cloned.1.call-start
  25.4 0.7 all-gather.2.cloned.1.call-update
  26.1 0.2 all-reduce.2.cloned.1.call-start
  26.4 25.3 %reduce-scatter.2.cloned.1.call-done = bf16[2048,1025]{0,1:T(8,128)(2,1)} async-done(((bf16[4096,1025]{0,1:T(8,128)(2,1)}), bf16[2048,1025]{0,1:T(8,128)(2,1)}) %reduce-scatter.2.cloned.1.call-update) | async-done | bytes 4198416 | tf_op jit(solution)/shard_map/reduce_scatter | solution.py:14
  51.7 4.8 %split.8 = bf16[2048,1024]{0,1:T(8,128)(2,1)} slice(bf16[2048,1025]{0,1:T(8,128)(2,1)} %reduce-scatter.2.cloned.1.call-done), slice={[0:2048], [0:1024]} | slice | bytes 8388608 | tf_op jit(solution)/shard_map/split | solution.py:15
  56.5 6.4 %copy.7 = bf16[2048,1024]{1,0:T(8,128)(2,1)} copy(bf16[2048,1024]{0,1:T(8,128)(2,1)} %split.8) | data formatting | bytes 8388608 | tf_op jit(solution)/shard_map/split | solution.py:15
  62.9 3.3 copy.8
  66.2 0.8 slice_reduce_fusion
  67.0 0.0 copy-start.1
  67.0 10.3 %maximum_convert_fusion = f32[2099200]{0:T(1024)} fusion(bf16[2048]{0:T(1024)(128)(2,1)S(1)} %slice_reduce_fusion, bf16[2097152]{0:T(1024)(128)(2,1)S(1)} %bitcast.5), kind=kLoop, calls=%fused_computation.8 | loop fusion | flops 8396800 | bytes 12595200 | tf_op jit(solution)/shard_map/concatenate | solution.py:25
  77.2 0.0 all-reduce.2.cloned.1.call-update
  77.3 0.0 copy-done.1
  77.3 0.3 multiply_reduce_fusion.1
  77.6 2.6 all-gather.2.cloned.1.call-done
  80.2 0.0 copy-start
  80.2 5.2 %multiply_reduce_fusion = f32[4096]{0:T(1024)S(1)} fusion(bf16[4096,1024]{1,0:T(8,128)(2,1)} %all-gather.2.cloned.1.call-done), kind=kLoop, calls=%fused_computation | loop fusion | flops 12578816 | bytes 8404992 | tf_op jit(solution)/shard_map/reduce_sum | solution.py:43
  85.4 0.5 copy-done
  85.9 5.1 %add_reduce_fusion = f32[512]{0:T(512)S(1)} fusion(bf16[512,1024]{1,0:T(8,128)(2,1)S(1)} %copy-done.1, bf16[4096,1024]{1,0:T(8,128)(2,1)S(1)} %copy-done, f32[4096]{0:T(1024)S(1)} %multiply_reduce_fusion, f32[512]{0:T(512)S(1)} %multiply_reduce_fusion.1), kind=kOutput, calls=%fused_computation.4 | convolution fusion | flops 4303355392 | bytes 9457664 | tf_op jit(solution)/shard_map/dot_general | solution.py:39
  91.0 0.6 broadcast_multiply_fusion
  91.6 256.4 %all-reduce.2.cloned.1.call-done = f32[2099200]{0:T(1024)} async-done(((f32[2099200]{0:T(1024)}), f32[2099200]{0:T(1024)}) %all-reduce.2.cloned.1.call-update) | async-done | bytes 8396816 | tf_op jit(solution)/shard_map/psum | solution.py:25
  348.0 5.9 %slice.20 = f32[2097152]{0:T(1024)} slice(f32[2099200]{0:T(1024)} %all-reduce.2.cloned.1.call-done), slice={[0:2097152]} | slice | bytes 16777216 | tf_op jit(solution)/shard_map/slice | solution.py:26
  353.9 9.3 %slice.18 = f32[2048,1024]{1,0:T(8,128)} reshape(f32[2097152]{0:T(1024)} %slice.20) | data formatting | bytes 16777216 | tf_op jit(solution)/shard_map/slice | solution.py:26
  363.1 0.7 slice_compare_fusion
  363.9 0.7 slice_maximum_fusion
  364.5 7.8 %convert_select_fusion = f32[2048,1024]{1,0:T(8,128)} fusion(bf16[2048,1024]{1,0:T(8,128)(2,1)} %param.5, f32[2048,1024]{1,0:T(8,128)} %slice.18, f32[2048]{0:T(1024)S(1)} %slice_maximum_fusion, pred[2048]{0:T(1024)(128)(4,1)S(1)} %slice_compare_fusion), kind=kLoop, calls=%fused_computation.5 | loop fusion | flops 6291456 | bytes 20981760 | tf_op jit(solution)/shard_map/jit(_where)/select_n | solution.py:31
  (1 shorter events, 0.0 us)
Async XLA Ops:
  7.2 44.5 %reduce-scatter.2.cloned.1.call-start = ((), (), s32[]{:S(2)}) async-start(), calls=%async_computation.1 | async-start | bytes 12681216 | tf_op jit(solution)/shard_map/reduce_scatter | solution.py:14
  25.4 54.8 %all-gather.2.cloned.1.call-start = ((), (), s32[]{:S(2)}) async-start(), calls=%async_computation.3 | async-start | bytes 12582912 | tf_op jit(solution)/shard_map/all_gather | solution.py:38
  26.1 321.9 %all-reduce.2.cloned.1.call-start = ((), (), s32[]{:S(2)}) async-start(), calls=%async_computation.2 | async-start | bytes 16793600 | tf_op jit(solution)/shard_map/psum | solution.py:25
  67.0 10.3 %copy-start.1 = (bf16[512,1024]{1,0:T(8,128)(2,1)S(1)}, bf16[512,1024]{1,0:T(8,128)(2,1)}, u32[]{:S(2)}) copy-start(bf16[512,1024]{1,0:T(8,128)(2,1)} %param.4) | copy-start | bytes 3145732
  80.2 5.8 %copy-start = (bf16[4096,1024]{1,0:T(8,128)(2,1)S(1)}, bf16[4096,1024]{1,0:T(8,128)(2,1)}, u32[]{:S(2)}) copy-start(bf16[4096,1024]{1,0:T(8,128)(2,1)} %all-gather.2.cloned.1.call-done) | copy-start | bytes 25165828
Sparse Core Ops, SparseCore 0:
  25.5 26.1 reduce-scatter.1
  53.5 26.6 all-gather.1
  85.8 262.1 all-reduce.1
where the time goes:
time: 380 us; the launch traced here: 379 us
  waiting for transfers between devices  285 us (75%)
  other arithmetic  35.6 us (9%)
  local copies, waits for them, and re-layouts  30.9 us (8%)
  between operations  13.8 us (4%)
  matrix products  13.1 us (3%)
    psum x1, waiting for transfers between devices, together(): total = lax.psum(jnp.concatenate([a.ravel() for a in arrays]), axis)  256 us
    reduce_scatter x1, waiting for transfers between devices, in_one_piece(): filled = lax.psum_scatter(both, axis, scatter_dimension=dim, tiled=True)  25.3 us
    slice x2, local copies, waits for them, and re-layouts, together(): total[b:e].reshape(a.shape)  15.1 us
    split x3, local copies, waits for them, and re-layouts, in_one_piece(): jnp.split(filled, [sum(widths[:k]) for k in range(1, len(widths))], axis=...  12 us
    concatenate x1, other arithmetic, together(): total = lax.psum(jnp.concatenate([a.ravel() for a in arrays]), axis)  10.3 us
    dot_general x1, matrix products, shards(): jnp.dot(onehot.astype(jnp.bfloat16), points, preferred_element_type=jnp.f...  8.07 us
    select_n x1, other arithmetic, update(): return jnp.where(counts[:, None] > 0.5, fresh, prior)  7.77 us
    concatenate x1, other arithmetic, in_one_piece(): jnp.concatenate([a.reshape(*a.shape[:along], w) for a, w in zip(arrays, w...  7.73 us
  transfers between devices with their start and end apart: 3, of which 3 were waited for; matrix products, arithmetic and copies ran while one was open for 10% of the time, Pallas kernels for 0%

commit v1 on v0

v1 whole, which is shorter than its diff:
```python
import jax
import jax.numpy as jnp
from jax import lax
from jax.experimental import pallas as pl
from jax.experimental.pallas import tpu as pltpu
from jax.sharding import Mesh
from jax.sharding import PartitionSpec as P

F32, BF16, I32 = jnp.float32, jnp.bfloat16, jnp.int32
LEVELS = 32767.0


def iota(shape, dim):
    return lax.broadcasted_iota(I32, shape, dim)


def sums_kernel(core_ref, x_ref, own_ref, send_ref):
    step = pl.program_id(0)

    @pl.when(step == 0)
    def _():
        own_ref[...] = jnp.zeros_like(own_ref)
        send_ref[...] = jnp.zeros_like(send_ref)

    core = core_ref[0]
    rows = x_ref.shape[2]
    digits = x_ref[0, 64:80, :].astype(F32)
    code = (digits[0:1] * 64.0 + digits[1:2]).astype(I32)
    low, high = code & 1023, code >> 10
    pick = (iota((1024, rows), 0) == low).astype(BF16)
    pts = x_ref[0, 0:64, :]
    masked = jnp.concatenate(
        [pts * (high == (b ^ (2 * core))).astype(BF16) for b in range(4)], axis=0
    )
    nt = (((1,), (1,)), ((), ()))
    part = lax.dot_general(pick, masked, nt, preferred_element_type=F32)
    own_ref[:, 0:128, :] += part[:, 0:128].reshape(8, 128, 128)
    send_ref[:, 0:128, :] += part[:, 128:256].reshape(8, 128, 128)
    slot = jnp.where(code < 4096, (low & 31) * 4 + high, -1)
    count_rows = (iota((32, rows), 0) == (low >> 5)).astype(BF16)
    count_cols = (iota((128, rows), 0) == slot).astype(BF16)
    counts = lax.dot_general(count_rows, count_cols, nt, preferred_element_type=F32)
    for z in range(8):
        own_ref[z, 128:132, :] += counts[z * 4 : z * 4 + 4]
        send_ref[z, 128:132, :] += counts[z * 4 : z * 4 + 4]


def partial_sums(core, x):
    return pl.pallas_call(
        sums_kernel,
        grid_spec=pltpu.PrefetchScalarGridSpec(
            num_scalar_prefetch=1,
            grid=(x.shape[0],),
            in_specs=[pl.BlockSpec((1, 80, 512), lambda s, c: (s, 0, 0))],
            out_specs=[pl.BlockSpec((8, 136, 128), lambda s, c: (0, 0, 0))] * 2,
        ),
        out_shape=[jax.ShapeDtypeStruct((8, 136, 128), F32)] * 2,
        compiler_params=pltpu.CompilerParams(dimension_semantics=("arbitrary",)),
        name="partial_sums",
    )(core, x)


def mean_kernel(core_ref, t_ref, prior_ref, w_ref):
    total = t_ref[0]
    for z in range(1, 8):
        total = total + t_ref[z]
    sums, counts = total[0:128], total[128:132]
    core = core_ref[0]
    row, lane = iota((128, 128), 0), iota((128, 128), 1)
    wide = jnp.concatenate([jnp.broadcast_to(counts[k : k + 1], (32, 128)) for k in range(4)], 0)
    wide = jnp.where((lane >> 2) == (row & 31), wide, 0.0)
    spread = ((row & 3) == (lane >> 6) + 2 * core).astype(F32)
    count = jnp.dot(wide, spread, precision=lax.Precision.HIGHEST, preferred_element_type=F32)
    mean = jnp.where(count > 0.5, sums / jnp.maximum(count, 1.0), prior_ref[...].astype(F32))
    peak = jnp.max(jnp.abs(mean), axis=0, keepdims=True)
    power = jnp.ceil(jnp.log2(jnp.maximum(peak, 1e-30)))
    q = jnp.round(mean * (LEVELS * jnp.exp2(-power)))
    q = jnp.clip(q, -LEVELS, LEVELS).astype(I32)
    w_ref[0:64, :] = (q[0:64] & 0xFFFF) | (q[64:128] << 16)
    w_ref[64:72, :] = jnp.broadcast_to(power.astype(I32), (8, 128))


def encoded_mean(core, t, prior):
    return pl.pallas_call(
        mean_kernel,
        in_specs=[
            pl.BlockSpec(memory_space=pltpu.SMEM),
            pl.BlockSpec(memory_space=pltpu.VMEM),
            pl.BlockSpec(memory_space=pltpu.VMEM),
        ],
        out_specs=pl.BlockSpec(memory_space=pltpu.VMEM),
        out_shape=jax.ShapeDtypeStruct((72, 128), I32),
        name="encoded_mean",
    )(core, t, prior)


def decode(block):
    packed = block[0:64]
    scale = jnp.exp2(block[64:65].astype(F32)) * (1.0 / LEVELS)
    first = ((packed << 16) >> 16).astype(F32) * scale
    second = (packed >> 16).astype(F32) * scale
    return first, second


def spread_kernel(a_ref, b_ref, out_ref):
    z = pl.program_id(0)
    left = iota((64, 128), 1) < 64

    def fill(block_of):
        for t in range(8):
            even = decode(block_of(2 * t))
            odd = decode(block_of(2 * t + 1))
            for h in range(2):
                e, o = even[h], odd[h]
                rows = slice(h * 64, h * 64 + 64)
                lanes = slice(t * 128, t * 128 + 128)
                out_ref[0, 0, rows, lanes] = jnp.where(left, e, pltpu.roll(o, 64, 1))
                out_ref[1, 0, rows, lanes] = jnp.where(left, pltpu.roll(e, 64, 1), o)

    @pl.when(z < 4)
    def _():
        fill(lambda yx: a_ref[yx % 4, yx // 4, 0])

    @pl.when(z >= 4)
    def _():
        fill(lambda yx: b_ref[yx // 4, yx % 4, 0])


def spread(a, b):
    return pl.pallas_call(
        spread_kernel,
        grid=(8,),
        in_specs=[
            pl.BlockSpec((4, 4, 1, 72, 128), lambda z: (0, 0, jnp.minimum(z, 3), 0, 0)),
            pl.BlockSpec((4, 4, 1, 72, 128), lambda z: (0, 0, jnp.maximum(z - 4, 0), 0, 0)),
        ],
        out_specs=pl.BlockSpec((2, 1, 128, 1024), lambda z: (0, z, 0, 0)),
        out_shape=jax.ShapeDtypeStruct((2, 8, 128, 1024), F32),
        compiler_params=pltpu.CompilerParams(dimension_semantics=("arbitrary",)),
        name="spread",
    )(a, b)


def gather(v, axis):
    size = lax.axis_size(axis)
    return lax.all_to_all(jnp.broadcast_to(v[None], (size,) + v.shape), axis, 0, 0)


def shards(points, centroids, assign, keep_mask):
    width = points.shape[1]
    swap = [(0, 1), (1, 0)]
    core = lax.axis_index("core").astype(I32)[None]
    other = lax.ppermute(centroids, "core", swap)

    code = jnp.where(keep_mask == 1, assign, 4096)
    digits = jnp.stack([code >> 6, code & 63]).astype(BF16)
    digits = jnp.concatenate([digits, jnp.zeros((14, 512), BF16)], axis=0)
    columns = points.T.reshape(16, 64, 512)
    x = jnp.concatenate([columns, jnp.broadcast_to(digits[None], (16, 16, 512))], axis=1)
    x = lax.all_to_all(x, ("y", "x"), 0, 0)

    own, send = partial_sums(core, x)
    t = own + lax.ppermute(send, "core", swap)
    t = lax.all_to_all(t, "z", 0, 0)
    plane = lax.axis_index("y") * 4 + lax.axis_index("x")
    prior = lax.dynamic_slice(
        centroids.reshape(2, 8, 128, width),
        (0, lax.axis_index("z"), 0, plane * 64),
        (2, 1, 128, 64),
    )
    prior = prior.reshape(2, 128, 64).transpose(1, 0, 2).reshape(128, 128)
    w = encoded_mean(core, t, prior)
    w = gather(w, "z")
    a = gather(gather(w[0:4], "y"), "x")
    b = gather(gather(w[4:8], "x"), "y")
    new_centroids = spread(a, b).reshape(2048, width)

    point_f = points.astype(F32)
    point_sq = jnp.sum(point_f * point_f, axis=1)

    def nearest(c):
        inner = lax.dot_general(
            points, c, (((1,), (1,)), ((), ())), preferred_element_type=F32
        )
        c_f = c.astype(F32)
        return jnp.min(jnp.sum(c_f * c_f, axis=1)[None, :] - 2.0 * inner, axis=1)

    row_cost = (point_sq + jnp.minimum(nearest(centroids), nearest(other))) / width
    return new_centroids, row_cost


def solution(mesh):
    grid = Mesh(mesh.devices.reshape(8, 4, 4, 2), ("z", "y", "x", "core"))
    rows = ("z", "y", "x", "core")
    in_specs = (P(rows, None), P("core", None), P(rows), P(rows))
    out_specs = (P("core", None), P(rows))
    return jax.shard_map(shards, mesh=grid, in_specs=in_specs, out_specs=out_specs, check_vma=False)
```

time: 380 us -> 198 us (0.52)
  waiting for transfers between devices: 285 us -> 73.4 us
  blocking collectives: 0 us -> 38.9 us
  starting transfers between devices: 0.3 us -> 27.5 us
  other arithmetic: 35.6 us -> 10.8 us
  Pallas kernels: 0 us -> 23.5 us
  local copies, waits for them, and re-layouts: 30.9 us -> 10.8 us
  between operations: 13.8 us -> 0.76 us
  matrix products: 13.1 us -> 9.29 us
    psum x1 -> x0, waiting for transfers between devices: 256 us -> none  [together(): total = lax.psum(jnp.concatenate([a.ravel() for a in arrays]), axis)]
    all_to_all x0 -> x4, waiting for transfers between devices: none -> 71.6 us  [the longest x2 36.4 us: gather(): lax.all_to_all(jnp.broadcast_to(v[None], (size,) + v.shape), axis, 0, 0)]
    all_to_all x0 -> x3, blocking collectives: none -> 38.9 us  [gather(): lax.all_to_all(jnp.broadcast_to(v[None], (size,) + v.shape), axis, 0, 0)]
    reduce_scatter x1 -> x0, waiting for transfers between devices: 25.3 us -> none  [in_one_piece(): filled = lax.psum_scatter(both, axis, scatter_dimension=dim, tiled=True)]
    all_to_all x0 -> x4, starting transfers between devices: none -> 23.9 us  [the longest x1 8.18 us: shards(): t = lax.all_to_all(t, 'z', 0, 0)]
    pallas_call x0 -> x3, Pallas kernels: none -> 23.5 us  [the longest x1 12.9 us: partial_sums(): pl.pallas_call(sums_kernel, grid_spec=pltpu.PrefetchScalarGridSpec(num_sc...]
    concatenate x2 -> x1, other arithmetic: 18 us -> 1.17 us  [shards(): jnp.concatenate([columns, jnp.broadcast_to(digits[None], (16, 16, 512))],...]
    slice x2 -> x1, local copies, waits for them, and re-layouts: 15.1 us -> 0.02 us  [shards(): b = gather(gather(w[4:8], 'x'), 'y')]
  transfers between devices with their start and end apart: 3 -> 6, of which waited for: 3 -> 5; matrix products, arithmetic and copies ran while one was open for 10% -> 12% of each run, Pallas kernels for 0% -> 1%
where the time goes in v1:
time: 198 us; the launch traced here: 195 us
  waiting for transfers between devices  73.4 us (37%)
  blocking collectives  38.9 us (20%)
  starting transfers between devices  27.5 us (14%)
  Pallas kernels  23.5 us (12%)
  other arithmetic  10.8 us (5%)
  local copies, waits for them, and re-layouts  10.8 us (5%)
  matrix products  9.29 us (5%)
    all_to_all x3, blocking collectives, gather(): lax.all_to_all(jnp.broadcast_to(v[None], (size,) + v.shape), axis, 0, 0)  38.9 us
    all_to_all x2, waiting for transfers between devices, gather(): lax.all_to_all(jnp.broadcast_to(v[None], (size,) + v.shape), axis, 0, 0)  36.4 us
    all_to_all x1, waiting for transfers between devices, shards(): x = lax.all_to_all(x, ('y', 'x'), 0, 0)  19 us
    all_to_all x1, waiting for transfers between devices, shards(): t = lax.all_to_all(t, 'z', 0, 0)  16.2 us
    pallas_call x1, Pallas kernels, partial_sums(): pl.pallas_call(sums_kernel, grid_spec=pltpu.PrefetchScalarGridSpec(num_sc...  12.9 us
    dot_general x2, matrix products, nearest(): lax.dot_general(points, c, (((1,), (1,)), ((), ())), preferred_element_ty...  9.29 us
    pallas_call x1, Pallas kernels, spread(): pl.pallas_call(spread_kernel, grid=(8,), in_specs=[pl.BlockSpec((4, 4, 1,...  8.69 us
    all_to_all x1, starting transfers between devices, shards(): t = lax.all_to_all(t, 'z', 0, 0)  8.18 us
  transfers between devices with their start and end apart: 6, of which 5 were waited for; matrix products, arithmetic and copies ran while one was open for 12% of the time, Pallas kernels for 1%

profile of v1, /device:TPU:1, one launch (start us, length us, event | category | flops | bytes accessed | tf_op | source)
XLA Modules:
  0.0 194.9 jit_solution(9686089787605776773)
XLA Ops:
  0.6 0.7 shift-right-arithmetic_convert_fusion
  1.3 1.5 copy.8
  2.9 1.2 pad_maximum_fusion
  4.1 7.6 %all-to-all-start = ((bf16[16,80,512]{2,1,0:T(8,128)(2,1)}), bf16[16,80,512]{2,1,0:T(8,128)(2,1)S(1)}, u32[]{:S(2)}, u32[]{:S(2)}) async-start(bf16[16,80,512]{2,1,0:T(8,128)(2,1)} %pad_maximum_fusion), calls=%async_computation | async-start | bytes 2621440 | tf_op jit(solution)/shard_map/all_to_all | solution.py:160
  11.7 19.0 %all-to-all-done.x_ref = bf16[16,80,512]{2,1,0:T(8,128)(2,1)S(1)} async-done(((bf16[16,80,512]{2,1,0:T(8,128)(2,1)}), bf16[16,80,512]{2,1,0:T(8,128)(2,1)S(1)}, u32[]{:S(2)}, u32[]{:S(2)}) %all-to-all-start) | async-done | bytes 1310752 | tf_op jit(solution)/shard_map/all_to_all | solution.py:160
  30.6 0.0 copy-start.1
  30.6 1.1 copy-done.1
  31.7 12.9 %partial_sums.1 = (f32[8,136,128]{2,1,0:T(8,128)}, f32[8,136,128]{2,1,0:T(8,128)}) custom-call(s32[1]{0:T(128)} %bitcast.core_ref, bf16[16,80,512]{2,1,0:T(8,128)(2,1)} %copy-done.1), custom_call_target="tpu_custom_call" | custom-call | tf_op jit(solution)/shard_map/partial_sums/pallas_call | solution.py:49
  44.6 2.9 %collective-permute-start = (f32[8,136,128]{2,1,0:T(8,128)}, f32[8,136,128]{2,1,0:T(8,128)S(1)}, u32[]{:S(2)}, u32[]{:S(2)}) collective-permute-start(f32[8,136,128]{2,1,0:T(8,128)} %get-tuple-element.5), channel_id=1, source_target_pairs={{0,1},{1,0},{2,3},{3,2},{4,5},{5,4},{6,7},{7,6},{8,9},{9,8},{10,11... | collective-permute-start | bytes 1671176 | tf_op jit(solution)/shard_map/ppermute | solution.py:163
  47.5 1.8 collective-permute-done
  49.3 1.9 add.17
  51.2 8.2 %all-to-all-start.1 = ((f32[8,136,128]{2,1,0:T(8,128)}), f32[8,136,128]{2,1,0:T(8,128)S(1)}, u32[]{:S(2)}, u32[]{:S(2)}) async-start(f32[8,136,128]{2,1,0:T(8,128)} %add.17), calls=%async_computation.1 | async-start | bytes 1114112 | tf_op jit(solution)/shard_map/all_to_all | solution.py:164
  59.4 0.7 collective-permute-start.1
  60.0 0.9 constant_dynamic-slice_fusion
  61.0 0.1 copy.11
  61.1 0.7 copy.10.prior_ref
  61.8 16.2 %all-to-all-done.1.t_ref = f32[8,136,128]{2,1,0:T(8,128)S(1)} async-done(((f32[8,136,128]{2,1,0:T(8,128)}), f32[8,136,128]{2,1,0:T(8,128)S(1)}, u32[]{:S(2)}, u32[]{:S(2)}) %all-to-all-start.1) | async-done | bytes 557088 | tf_op jit(solution)/shard_map/all_to_all | solution.py:164
  78.0 0.0 copy-start.3
  78.0 0.8 copy-done.3
  78.8 1.9 encoded_mean.1
  80.8 0.8 broadcast_in_dim.21
  81.5 15.1 %all_to_all.35 = s32[8,72,128]{2,1,0:T(8,128)S(1)} all-to-all(s32[8,72,128]{2,1,0:T(8,128)S(1)} %broadcast_in_dim.21), channel_id=1, replica_groups=mesh['z'=8,'y'=4,'x'=4,'core'=2] {'z'}, dimensions={0} | all-to-all | bytes 589824 | tf_op jit(solution)/shard_map/all_to_all | solution.py:146
  96.8 11.9 %all_to_all.36 = s32[4,4,72,128]{3,2,1,0:T(8,128)S(1)} all-to-all(s32[4,4,72,128]{3,2,1,0:T(8,128)S(1)} %broadcast_in_dim.22), channel_id=1, replica_groups=mesh['z'=8,'y'=4,'x'=4,'core'=2] {'y'}, dimensions={0} | all-to-all | bytes 1179648 | tf_op jit(solution)/shard_map/all_to_all | solution.py:146
  108.7 0.0 copy-start.2
  108.7 11.9 %all_to_all.37 = s32[4,4,72,128]{3,2,1,0:T(8,128)} all-to-all(s32[4,4,72,128]{3,2,1,0:T(8,128)S(1)} %broadcast_in_dim.24), channel_id=1, replica_groups=mesh['z'=8,'y'=4,'x'=4,'core'=2] {'x'}, dimensions={0} | all-to-all | bytes 1179648 | tf_op jit(solution)/shard_map/all_to_all | solution.py:146
  120.6 1.6 broadcast_in_dim.23
  122.3 3.6 %all-to-all-start.4 = ((s32[4,4,4,72,128]{4,3,2,1,0:T(8,128)}), s32[4,4,4,72,128]{4,3,2,1,0:T(8,128)S(1)}, u32[]{:S(2)}, u32[]{:S(2)}) async-start(s32[4,4,4,72,128]{4,3,2,1,0:T(8,128)} %broadcast_in_dim.23), calls=%async_computation.4 | async-start | bytes 4718592 | tf_op jit(solution)/shard_map/all_to_all | solution.py:146
  125.9 0.0 copy-done.2
  125.9 0.3 multiply_reduce_fusion.2
  126.2 3.1 %multiply_reduce_fusion.1 = f32[2048]{0:T(1024)S(1)} fusion(bf16[2048,1024]{1,0:T(8,128)(2,1)} %param.5), kind=kLoop, calls=%fused_computation.1 | loop fusion | flops 6289408 | bytes 4202496 | tf_op jit(solution)/shard_map/reduce_sum | solution.py:186
  129.3 23.4 %all-to-all-done.4.a_ref = s32[4,4,4,72,128]{4,3,2,1,0:T(8,128)S(1)} async-done(((s32[4,4,4,72,128]{4,3,2,1,0:T(8,128)}), s32[4,4,4,72,128]{4,3,2,1,0:T(8,128)S(1)}, u32[]{:S(2)}, u32[]{:S(2)}) %all-to-all-start.4) | async-done | bytes 2359328 | tf_op jit(solution)/shard_map/all_to_all | solution.py:146
  152.6 0.0 copy-start
  152.6 3.1 %broadcast_in_dim.25 = s32[4,4,4,72,128]{4,3,2,1,0:T(8,128)} broadcast(s32[4,4,72,128]{3,2,1,0:T(8,128)} %all_to_all.37), dimensions={1,2,3,4} | broadcast | bytes 2949120 | tf_op jit(solution)/shard_map/broadcast_in_dim | solution.py:146
  155.7 4.5 %all-to-all-start.6 = ((s32[4,4,4,72,128]{4,3,2,1,0:T(8,128)}), s32[4,4,4,72,128]{4,3,2,1,0:T(8,128)}, u32[]{:S(2)}, u32[]{:S(2)}) async-start(s32[4,4,4,72,128]{4,3,2,1,0:T(8,128)} %broadcast_in_dim.25), calls=%async_computation.6 | async-start | bytes 4718592 | tf_op jit(solution)/shard_map/all_to_all | solution.py:146
  160.2 4.7 %subtract_reduce_fusion.1 = f32[512]{0:T(512)S(1)} fusion(bf16[512,1024]{1,0:T(8,128)(2,1)S(1)} %copy-done.2, bf16[2048,1024]{1,0:T(8,128)(2,1)} %param.5, f32[2048]{0:T(1024)S(1)} %multiply_reduce_fusion.1), kind=kOutput, calls=%fused_computation.3 | convolution fusion | flops 2150628864 | bytes 5253120 | tf_op jit(solution)/shard_map/dot_general | solution.py:182
  164.9 0.0 copy-done
  164.9 0.0 collective-permute-done.1
  164.9 3.1 %multiply_reduce_fusion = f32[2048]{0:T(1024)S(1)} fusion(bf16[2048,1024]{1,0:T(8,128)(2,1)} %collective-permute-done.1), kind=kLoop, calls=%fused_computation | loop fusion | flops 6289408 | bytes 4202496 | tf_op jit(solution)/shard_map/reduce_sum | solution.py:186
  168.0 4.6 %subtract_reduce_fusion = f32[512]{0:T(512)S(1)} fusion(f32[2048]{0:T(1024)S(1)} %multiply_reduce_fusion, bf16[512,1024]{1,0:T(8,128)(2,1)S(1)} %copy-done.2, bf16[2048,1024]{1,0:T(8,128)(2,1)} %collective-permute-done.1), kind=kOutput, calls=%fused_computation.2 | convolution fusion | flops 2150628864 | bytes 5253120 | tf_op jit(solution)/shard_map/dot_general | solution.py:182
  172.6 0.6 add_multiply_fusion
  173.2 13.0 %all-to-all-done.6.b_ref = s32[4,4,4,72,128]{4,3,2,1,0:T(8,128)} async-done(((s32[4,4,4,72,128]{4,3,2,1,0:T(8,128)}), s32[4,4,4,72,128]{4,3,2,1,0:T(8,128)}, u32[]{:S(2)}, u32[]{:S(2)}) %all-to-all-start.6) | async-done | bytes 2359328 | tf_op jit(solution)/shard_map/all_to_all | solution.py:146
  186.2 8.7 %spread.1 = f32[2,8,128,1024]{3,2,1,0:T(8,128)} custom-call(s32[4,4,4,72,128]{4,3,2,1,0:T(8,128)} %copy-done, s32[4,4,4,72,128]{4,3,2,1,0:T(8,128)} %all-to-all-done.6.b_ref), custom_call_target="tpu_custom_call" | custom-call | tf_op jit(solution)/shard_map/spread/pallas_call | solution.py:130
  (7 shorter events, 0.1 us)
Async XLA Ops:
  4.1 26.5 %all-to-all-start = ((bf16[16,80,512]{2,1,0:T(8,128)(2,1)}), bf16[16,80,512]{2,1,0:T(8,128)(2,1)S(1)}, u32[]{:S(2)}, u32[]{:S(2)}) async-start(bf16[16,80,512]{2,1,0:T(8,128)(2,1)} %pad_maximum_fusion), calls=%async_computation | async-start | bytes 2621440 | tf_op jit(solution)/shard_map/all_to_all | solution.py:160
  30.6 1.1 copy-start.1
  44.6 4.7 %collective-permute-start = (f32[8,136,128]{2,1,0:T(8,128)}, f32[8,136,128]{2,1,0:T(8,128)S(1)}, u32[]{:S(2)}, u32[]{:S(2)}) collective-permute-start(f32[8,136,128]{2,1,0:T(8,128)} %get-tuple-element.5), channel_id=1, source_target_pairs={{0,1},{1,0},{2,3},{3,2},{4,5},{5,4},{6,7},{7,6},{8,9},{9,8},{10,11... | collective-permute-start | bytes 1671176 | tf_op jit(solution)/shard_map/ppermute | solution.py:163
  51.2 26.8 %all-to-all-start.1 = ((f32[8,136,128]{2,1,0:T(8,128)}), f32[8,136,128]{2,1,0:T(8,128)S(1)}, u32[]{:S(2)}, u32[]{:S(2)}) async-start(f32[8,136,128]{2,1,0:T(8,128)} %add.17), calls=%async_computation.1 | async-start | bytes 1114112 | tf_op jit(solution)/shard_map/all_to_all | solution.py:164
  59.4 105.5 %collective-permute-start.1 = (bf16[2048,1024]{1,0:T(8,128)(2,1)}, bf16[2048,1024]{1,0:T(8,128)(2,1)}, u32[]{:S(2)}, u32[]{:S(2)}) collective-permute-start(bf16[2048,1024]{1,0:T(8,128)(2,1)} %param.5), channel_id=1, source_target_pairs={{0,1},{1,0},{2,3},{3,2},{4,5},{5,4},{6,7},{7,6},{8,9},{9,8},{10,11... | collective-permute-start | bytes 12582920 | tf_op jit(solution)/shard_map/ppermute | solution.py:153
  78.0 0.8 copy-start.3
  108.7 17.2 %copy-start.2 = (bf16[512,1024]{1,0:T(8,128)(2,1)S(1)}, bf16[512,1024]{1,0:T(8,128)(2,1)}, u32[]{:S(2)}) copy-start(bf16[512,1024]{1,0:T(8,128)(2,1)} %param.4) | copy-start | bytes 3145732
  122.3 30.4 %all-to-all-start.4 = ((s32[4,4,4,72,128]{4,3,2,1,0:T(8,128)}), s32[4,4,4,72,128]{4,3,2,1,0:T(8,128)S(1)}, u32[]{:S(2)}, u32[]{:S(2)}) async-start(s32[4,4,4,72,128]{4,3,2,1,0:T(8,128)} %broadcast_in_dim.23), calls=%async_computation.4 | async-start | bytes 4718592 | tf_op jit(solution)/shard_map/all_to_all | solution.py:146
  152.6 12.3 %copy-start = (s32[4,4,4,72,128]{4,3,2,1,0:T(8,128)}, s32[4,4,4,72,128]{4,3,2,1,0:T(8,128)S(1)}, u32[]{:S(2)}) copy-start(s32[4,4,4,72,128]{4,3,2,1,0:T(8,128)S(1)} %all-to-all-done.4.a_ref) | copy-start | bytes 7077892
  155.7 30.5 %all-to-all-start.6 = ((s32[4,4,4,72,128]{4,3,2,1,0:T(8,128)}), s32[4,4,4,72,128]{4,3,2,1,0:T(8,128)}, u32[]{:S(2)}, u32[]{:S(2)}) async-start(s32[4,4,4,72,128]{4,3,2,1,0:T(8,128)} %broadcast_in_dim.25), calls=%async_computation.6 | async-start | bytes 4718592 | tf_op jit(solution)/shard_map/all_to_all | solution.py:146
